TPU v7x, 32 devices: a whole 2x2x4 slice. The times are simulated.
32 devices in a mesh: dp: 4 (over z), fsdp: 8 (over y, x, core).
Axes of the slice: x: 2, y: 2, z: 4, core: 2. Of those that a mesh axis runs over, the one named last changes fastest.
Arguments:
- replica_grads: bfloat16 [4, 8192, 4096], P('dp', 'fsdp'), may hold values from -4 to 4
- slot_table: int32 [32], replicated, may hold values from 0 to 39, as said below
- left_gram_state: float32 [40, 1, 4, 256, 1024], P('fsdp', None, 'dp')
- right_gram_state: float32 [40, 1, 4, 256, 1024], P('fsdp', None, 'dp')
- left_inverse_root: bfloat16 [40, 1, 4, 256, 1024], P('fsdp', None, 'dp')
- right_inverse_root: bfloat16 [40, 1, 4, 256, 1024], P('fsdp', None, 'dp')
Outputs:
- direction: bfloat16 [8, 4, 256, 4096], P('fsdp', 'dp')
- left_new: float32 [40, 1, 4, 256, 1024], P('fsdp', None, 'dp')
- right_new: float32 [40, 1, 4, 256, 1024], P('fsdp', None, 'dp')
Inputs may be any that keep to these rules, and one draw needn't show every extreme that they name: `slot_table`: the entries are distinct; slot v belongs to owner v // 5 of the flat shards' devices; some owner holds 5 blocks.
All inputs are finite; a program needn't handle non-finite values.
Results may differ from a plain program's by a relative error of at most 0.02.
Values may be sent and summed in bfloat16 or wider, within the bound.
A program may use at most 192 MiB of HBM per device.

v0:
```python
import jax
import jax.numpy as jnp
from jax import lax
from jax.sharding import PartitionSpec as P


def on_device(
    replica_grads,
    slot_table,
    left_gram_state,
    right_gram_state,
    left_inverse_root,
    right_inverse_root,
):
    slots_here = left_gram_state.shape[0]
    sub_blocks = left_gram_state.shape[1]
    strip_rows = left_gram_state.shape[3]
    block_size = left_gram_state.shape[4]
    band_rows = replica_grads.shape[1]
    model_width = replica_grads.shape[2]
    per_band = model_width // block_size
    shards = lax.axis_size("fsdp")
    groups = lax.axis_size("dp")
    total_slots = shards * slots_here
    block_count = slot_table.shape[0]
    band_index = lax.axis_index("fsdp")
    strip_index = lax.axis_index("dp")
    slot_indices = jnp.arange(total_slots, dtype=jnp.int32)
    summed = lax.psum_scatter(
        replica_grads[0].astype(jnp.float32).astype(jnp.bfloat16),
        "dp",
        scatter_dimension=0,
        tiled=True,
    )
    row_block = band_index * band_rows // block_size
    targets = lax.dynamic_slice_in_dim(slot_table, row_block * per_band, per_band, 0)
    chooser = (targets[:, None] == slot_indices[None, :]).astype(jnp.bfloat16)
    own_slots = band_index * slots_here + jnp.arange(slots_here, dtype=jnp.int32)
    holder = slot_table[None, :] == own_slots[:, None]
    occupied = jnp.any(holder, axis=1)
    block_of = jnp.sum(
        jnp.where(holder, jnp.arange(block_count, dtype=jnp.int32)[None, :], 0), axis=1
    )
    first_band = block_of // per_band * sub_blocks
    col_block = block_of % per_band
    all_bands = lax.all_gather(summed[None], "fsdp", axis=0, tiled=True)
    owned_rows = jax.vmap(
        lambda offset, column: lax.dynamic_slice(
            all_bands, (offset, 0, column * block_size), (sub_blocks, strip_rows, block_size)
        )
    )(first_band, col_block)
    owned_rows = owned_rows * occupied[:, None, None, None].astype(jnp.bfloat16)
    owned_rows = owned_rows.reshape(slots_here, sub_blocks, 1, strip_rows, block_size)
    entire = lax.all_gather(owned_rows, "dp", axis=2, tiled=True).reshape(
        slots_here, block_size, block_size
    )
    my_rows = owned_rows.reshape(slots_here, sub_blocks * strip_rows, block_size)
    left_gram = jnp.einsum("mrc,mnc->mrn", my_rows, entire, preferred_element_type=jnp.float32)
    left_new = left_gram_state + (left_gram / block_size).reshape(left_gram_state.shape)
    my_columns = lax.dynamic_index_in_dim(
        entire.reshape(slots_here, block_size, sub_blocks, groups, strip_rows),
        strip_index,
        3,
        keepdims=False,
    )
    my_columns = my_columns.reshape(slots_here, block_size, sub_blocks * strip_rows)
    right_gram = jnp.einsum("mnr,mnc->mrc", my_columns, entire, preferred_element_type=jnp.float32)
    right_new = right_gram_state + (right_gram / block_size).reshape(right_gram_state.shape)
    left_rows = left_inverse_root.reshape(slots_here, sub_blocks * strip_rows, block_size)
    mixed_rows = jnp.einsum(
        "mrn,mnc->mrc", left_rows, entire, preferred_element_type=jnp.float32
    ).astype(jnp.bfloat16)
    mixed_split = mixed_rows.reshape(
        slots_here, sub_blocks * strip_rows, sub_blocks, groups, strip_rows
    )
    result = jnp.einsum(
        "mrqjt,mqjtc->mrc",
        mixed_split,
        lax.all_gather(right_inverse_root, "dp", axis=2, tiled=True),
        preferred_element_type=jnp.float32,
    )
    outcome = result.astype(jnp.bfloat16).reshape(slots_here, sub_blocks, strip_rows, block_size)
    homeward = jax.vmap(
        lambda portion, offset: lax.dynamic_update_slice_in_dim(
            jnp.zeros((shards, strip_rows, block_size), jnp.bfloat16), portion, offset, 0
        ),
        out_axes=1,
    )(outcome, first_band)
    returned = lax.all_to_all(homeward, "fsdp", split_axis=0, concat_axis=0, tiled=True)
    picked = jnp.einsum(
        "cn,ntb->tcb",
        chooser,
        returned.reshape(total_slots, strip_rows, block_size),
        preferred_element_type=jnp.float32,
    ).astype(jnp.bfloat16)
    direction = picked.reshape(1, 1, strip_rows, model_width)
    return (direction, left_new, right_new)


def solution(mesh):
    placed = (
        P("dp", "fsdp", None),
        P(),
        P("fsdp", None, "dp", None, None),
        P("fsdp", None, "dp", None, None),
        P("fsdp", None, "dp", None, None),
        P("fsdp", None, "dp", None, None),
    )
    return jax.shard_map(
        on_device,
        mesh=mesh,
        in_specs=placed,
        out_specs=(
            P("fsdp", "dp", None, None),
            P("fsdp", None, "dp", None, None),
            P("fsdp", None, "dp", None, None),
        ),
        check_vma=False,
    )
```

profile of v0, /device:TPU:1, one launch (start us, length us, event | category | flops | bytes accessed | tf_op | source)
XLA Modules:
  0.0 972.9 jit_solution(10129963581104067872)
XLA Ops:
  7.2 0.7 reduce-scatter.2.cloned.1.call-update
  8.0 148.7 %reduce-scatter.2.cloned.1.call-done = bf16[256,4096]{1,0:T(8,128)(2,1)} async-done(((bf16[1024,4096]{1,0:T(8,128)(2,1)}), bf16[256,4096]{1,0:T(8,128)(2,1)}) %reduce-scatter.2.cloned.1.call-update) | async-done | bytes 2097168 | tf_op jit(solution)/shard_map/reduce_scatter | solution.py:29
  156.8 0.2 compare_reduce_fusion
  157.0 0.2 fusion.22
  157.2 0.1 fusion.23
  157.3 92.5 %all-gather.9.cloned.1.call-done = bf16[2048,4096]{1,0:T(8,128)(2,1)} async-done(((bf16[256,4096]{1,0:T(8,128)(2,1)}), bf16[2048,4096]{1,0:T(8,128)(2,1)}) %all-gather.9.cloned.1.call-update) | async-done | bytes 16777232 | tf_op jit(solution)/shard_map/all_gather | solution.py:46
  249.7 19.4 %while.2 = (s32[]{:T(128)}, bf16[8,256,4096]{2,1,0:T(8,128)(2,1)}, s32[5,3]{0,1:T(4,128)S(1)}, bf16[5,1,256,1024]{3,2,1,0:T(8,128)(2,1)}, s32[]{:T(128)}) while((s32[]{:T(128)}, bf16[8,256,4096]{2,1,0:T(8,128)(2,1)}, s32[5,3]{0,1:T(4,128)S(1)}, bf16[5,1,256,1024]{3,2,1,0:T(8,128)(2,1)}, s32[]{:T(128)}) %tuple.63), condition=%wide.while_cond, body=%wide.while_body.sunk | while | flops 2 | bytes 1049717 | solution.py:48
  249.7 0.1 constant_dynamic-slice_fusion.7
  249.8 0.5 fusion.36
  250.3 3.3 bitcast_dynamic-update-slice_fusion.4
  253.6 0.1 constant_dynamic-slice_fusion.7
  253.7 0.5 fusion.36
  254.2 3.3 bitcast_dynamic-update-slice_fusion.4
  257.5 0.1 constant_dynamic-slice_fusion.7
  257.6 0.5 fusion.36
  258.1 3.3 bitcast_dynamic-update-slice_fusion.4
  261.4 0.1 constant_dynamic-slice_fusion.7
  261.5 0.5 fusion.36
  262.0 3.3 bitcast_dynamic-update-slice_fusion.4
  265.3 0.1 constant_dynamic-slice_fusion.7
  265.3 0.5 fusion.36
  265.9 3.3 bitcast_dynamic-update-slice_fusion.4
  269.2 3.5 bitcast_multiply_fusion.2
  272.7 0.5 all-gather.7.cloned.1.call-update
  273.3 183.2 %all-gather.5.cloned.1.call-done = bf16[5,1,4,256,1024]{4,3,1,0,2:T(8,128)(2,1)} async-done(((bf16[5,1,1,256,1024]{4,3,1,0,2:T(8,128)(2,1)}), bf16[5,1,4,256,1024]{4,3,1,0,2:T(8,128)(2,1)}) %all-gather.5.cloned.1.call-update) | async-done | bytes 10485776 | tf_op jit(solution)/shard_map/all_gather | solution.py:54
  456.5 17.3 %copy.48 = bf16[5,1,4,256,1024]{3,2,4,0,1:T(4,128)(2,1)} copy(bf16[5,1,4,256,1024]{4,3,1,0,2:T(8,128)(2,1)} %all-gather.5.cloned.1.call-done) | data formatting | bytes 20971520 | tf_op jit(solution)/shard_map/all_gather | solution.py:54
  473.8 17.6 %reshape.158 = bf16[5,1024,1024]{1,2,0:T(8,128)(2,1)} reshape(bf16[5,1,4,256,1024]{3,2,4,0,1:T(4,128)(2,1)} %copy.48) | data formatting | bytes 20971520 | tf_op jit(solution)/shard_map/reshape | solution.py:54
  491.4 8.4 fusion.16
  499.8 140.2 %all-gather.7.cloned.1.call-done = bf16[5,1,4,256,1024]{4,3,2,0,1:T(8,128)(2,1)} async-done(((bf16[5,1,1,256,1024]{4,3,2,0,1:T(8,128)(2,1)}), bf16[5,1,4,256,1024]{4,3,2,0,1:T(8,128)(2,1)}) %all-gather.7.cloned.1.call-update) | async-done | bytes 10485776 | tf_op jit(solution)/shard_map/all_gather | solution.py:79
  640.0 9.3 fusion.6
  649.3 7.4 broadcast_in_dim.18.clone
  656.7 52.1 %while.3 = (s32[]{:T(128)}, bf16[5,8,256,1024]{3,2,0,1:T(8,128)(2,1)}, s32[5,4]{0,1:T(4,128)S(1)}, bf16[5,1,256,1024]{3,2,1,0:T(8,128)(2,1)}, s32[]{:T(128)}, /*index=5*/s32[4]{0:T(128)S(1)}) while((s32[]{:T(128)}, bf16[5,8,256,1024]{3,2,0,1:T(8,128)(2,1)}, s32[5,4]{0,1:T(4,128)S(1)}, bf16[5,1,256,1024]{3,2,1,0:T(8,128)(2,1)}, s32[]{:T(128)}, ...), condition=%wide.while_cond.1, body=%wide.while_body.1.sunk | while | flops 262173 | bytes 2623166 | solution.py:84
  656.7 0.1 constant_dynamic-slice_fusion.8
  656.7 0.6 fusion.37
  657.3 3.3 and_reduce_fusion.2
  660.7 2.4 constant_dynamic-slice_fusion.9
  663.1 4.0 bitcast_dynamic-update-slice_fusion.5
  667.1 0.6 fusion.37
  667.7 3.3 and_reduce_fusion.2
  671.1 2.4 constant_dynamic-slice_fusion.9
  673.5 4.0 bitcast_dynamic-update-slice_fusion.5
  677.5 0.6 fusion.37
  678.1 3.3 and_reduce_fusion.2
  681.5 2.4 constant_dynamic-slice_fusion.9
  683.9 4.0 bitcast_dynamic-update-slice_fusion.5
  688.0 0.6 fusion.37
  688.6 3.3 and_reduce_fusion.2
  691.9 2.4 constant_dynamic-slice_fusion.9
  694.4 4.0 bitcast_dynamic-update-slice_fusion.5
  698.4 0.6 fusion.37
  699.0 3.3 and_reduce_fusion.2
  702.3 2.4 constant_dynamic-slice_fusion.9
  704.8 4.0 bitcast_dynamic-update-slice_fusion.5
  708.7 6.5 all-to-all-start
  715.2 0.1 dynamic_slice.7
  715.3 9.7 copy.56
  724.9 17.9 %reshape_reshape.4 = bf16[5,1024,1,4,256]{4,3,1,0,2:T(4,128)(2,1)} reshape(bf16[5,1,4,256,1024]{4,3,2,0,1:T(8,128)(2,1)} %copy.56) | data formatting | bytes 20971520 | tf_op jit(solution)/shard_map/reshape;reshape | solution.py:61
  742.8 8.7 constant_dynamic-slice_fusion.3
  751.5 11.1 %copy.57 = bf16[5,1024,1,1,256]{1,4,0,3,2:T(8,128)(2,1)} copy(bf16[5,1024,1,1,256]{4,3,1,0,2:T(2,128)(2,1)} %constant_dynamic-slice_fusion.3) | data formatting | bytes 5242880 | tf_op jit(solution)/shard_map/jit(dynamic_index_in_dim)/dynamic_slice | solution.py:60
  762.6 11.7 %fusion.4 = f32[5,1,1,256,1024]{4,3,2,1,0:T(8,128)} fusion(f32[5,1,1,256,1024]{4,3,2,1,0:T(8,128)} %param.9, bf16[5,1024,1024]{1,2,0:T(8,128)(2,1)} %reshape.158, bf16[5,1024,1,1,256]{1,4,0,3,2:T(8,128)(2,1)} %copy.57), kind=kOutput, calls=%fused_computation.12 | convolution fusion | flops 2686976000 | bytes 23592960 | tf_op jit(solution)/shard_map/mnr,mnc->mrc/dot_general | solution.py:67
  774.3 9.6 fusion.5
  783.8 156.6 %all-to-all-done = bf16[8,5,256,1024]{3,2,1,0:T(8,128)(2,1)} async-done(((bf16[8,5,256,1024]{3,2,1,0:T(8,128)(2,1)}), bf16[8,5,256,1024]{3,2,1,0:T(8,128)(2,1)}, u32[]{:S(2)}, u32[]{:S(2)}) %all-to-all-start) | async-done | bytes 20971552 | tf_op jit(solution)/shard_map/all_to_all | solution.py:89
  940.4 21.6 %convert_bitcast_fusion = bf16[256,4,1024]{2,1,0:T(4,128)(2,1)} fusion(bf16[40,256,1024]{2,1,0:T(8,128)(2,1)} %bitcast.14, s32[4]{0:T(128)S(1)} %dynamic_slice.7), kind=kOutput, calls=%fused_computation.24 | convolution fusion | flops 84934816 | bytes 23068688 | tf_op jit(solution)/shard_map/cn,ntb->tcb/dot_general | solution.py:90
  962.0 4.5 reshape.164
  (29 shorter events, 0.6 us)
Async XLA Ops:
  7.2 484.2 %copy-start = (bf16[5,1,1,256,1024]{4,3,2,1,0:T(8,128)(2,1)S(1)}, bf16[5,1,1,256,1024]{4,3,2,1,0:T(8,128)(2,1)}, u32[]{:S(2)}) copy-start(bf16[5,1,1,256,1024]{4,3,2,1,0:T(8,128)(2,1)} %param.10) | copy-start | bytes 7864324
  7.2 149.5 %reduce-scatter.2.cloned.1.call-start = ((), (), s32[]{:S(2)}) async-start(), calls=%async_computation.2 | async-start | bytes 10485760 | tf_op jit(solution)/shard_map/reduce_scatter | solution.py:29
  7.2 149.5 %copy-start.5 = (s32[32]{0:T(128)S(1)}, s32[32]{0:T(128)}, u32[]{:S(2)}) copy-start(s32[32]{0:T(128)} %param.7) | copy-start | bytes 388
  7.2 150.0 %copy-start.4 = (s32[3]{0:T(128)S(1)}, s32[3]{0:T(128)}, u32[]{:S(2)}) copy-start(s32[3]{0:T(128)} %constant.68.clone.1) | copy-start | bytes 40
  7.9 241.8 %all-gather.9.cloned.1.call-start = ((), (), s32[]{:S(2)}) async-start(), calls=%async_computation.5 | async-start | bytes 18874368 | tf_op jit(solution)/shard_map/all_gather | solution.py:46
  156.7 299.8 %all-gather.5.cloned.1.call-start = ((), (), s32[]{:S(2)}) async-start(), calls=%async_computation.3 | async-start | bytes 13107200 | tf_op jit(solution)/shard_map/all_gather | solution.py:54
  272.7 367.3 %all-gather.7.cloned.1.call-start = ((), (), s32[]{:S(2)}) async-start(), calls=%async_computation.4 | async-start | bytes 13107200 | tf_op jit(solution)/shard_map/all_gather | solution.py:79
  649.3 7.4 copy-start.3
  708.7 231.7 %all-to-all-start = ((bf16[8,5,256,1024]{3,2,1,0:T(8,128)(2,1)}), bf16[8,5,256,1024]{3,2,1,0:T(8,128)(2,1)}, u32[]{:S(2)}, u32[]{:S(2)}) async-start(bf16[8,5,256,1024]{3,2,1,0:T(8,128)(2,1)} %bitcast.125), calls=%async_computation.1 | async-start | bytes 41943040 | tf_op jit(solution)/shard_map/all_to_all | solution.py:89
  762.6 11.7 %copy-start.2 = (bf16[5,1,256,1024]{3,2,1,0:T(8,128)(2,1)S(1)}, bf16[5,1,256,1024]{3,2,1,0:T(8,128)(2,1)}, u32[]{:S(2)}) copy-start(bf16[5,1,256,1024]{3,2,1,0:T(8,128)(2,1)} %get-tuple-element.10) | copy-start | bytes 7864324
  940.4 26.0 %copy-start.1 = (bf16[5,1,1,256,1024]{4,3,2,1,0:T(8,128)(2,1)S(1)}, bf16[5,1,1,256,1024]{4,3,2,1,0:T(8,128)(2,1)}, u32[]{:S(2)}) copy-start(bf16[5,1,1,256,1024]{4,3,2,1,0:T(8,128)(2,1)} %param.10) | copy-start | bytes 7864324
Sparse Core Ops, SparseCore 0:
  10.3 146.2 reduce-scatter.1
  158.6 91.1 all-gather.8
  272.8 183.6 all-gather.4
  457.9 182.0 all-gather.6
where the time goes:
time: 980 us; the launch traced here: 973 us
  waiting for transfers between devices  722 us (74%)
  local copies, waits for them, and re-layouts  129 us (13%)
  matrix products  60.5 us (6%)
  other arithmetic  40.4 us (4%)
  between operations  13.9 us (1%)
    all_gather x1, waiting for transfers between devices, on_device(): lax.all_gather(owned_rows, 'dp', axis=2, tiled=True)  183 us
    all_to_all x1, waiting for transfers between devices, on_device(): lax.all_to_all(homeward, 'fsdp', split_axis=0, concat_axis=0, tiled=True)  157 us
    reduce_scatter x1, waiting for transfers between devices, on_device(): lax.psum_scatter(replica_grads[0].astype(jnp.float32).astype(jnp.bfloat16...  149 us
    all_gather x1, waiting for transfers between devices, on_device(): lax.all_gather(right_inverse_root, 'dp', axis=2, tiled=True)  140 us
    all_gather x1, waiting for transfers between devices, on_device(): all_bands = lax.all_gather(summed[None], 'fsdp', axis=0, tiled=True)  92.5 us
    scatter x10, other arithmetic  36.5 us
    all_gather x2, local copies, waits for them, and re-layouts, on_device(): lax.all_gather(owned_rows, 'dp', axis=2, tiled=True)  27 us
    dot_general x1, matrix products, on_device(): jnp.einsum('cn,ntb->tcb', chooser, returned.reshape(total_slots, strip_ro...  21.6 us
  transfers between devices with their start and end apart: 5, of which 5 were waited for; matrix products, arithmetic and copies ran while one was open for 12% of the time, Pallas kernels for 0%

commit v1 on v0

--- a/solution.py
+++ b/solution.py
@@ -1,7 +1,338 @@
+import functools
+
 import jax
 import jax.numpy as jnp
 from jax import lax
+from jax.experimental import pallas as pl
+from jax.experimental.pallas import tpu as pltpu
 from jax.sharding import PartitionSpec as P
+
+MESH = pl.DeviceIdType.MESH
+ANY = pl.BlockSpec(memory_space=pl.ANY)
+VMEM = pl.BlockSpec(memory_space=pltpu.VMEM)
+SMEM = pl.BlockSpec(memory_space=pltpu.SMEM)
+F32 = jnp.float32
+BF16 = jnp.bfloat16
+
+
+def greet(peers):
+    barrier = pltpu.get_barrier_semaphore()
+    for peer in peers:
+        pl.semaphore_signal(barrier, inc=1, device_id=peer, device_id_type=MESH)
+    pl.semaphore_wait(barrier, len(peers))
+
+
+def scatter_kernel(groups, shards, x_ref, o_ref, send_sem, recv_sem, own_sem):
+    z, f = lax.axis_index("dp"), lax.axis_index("fsdp")
+    peers = []
+    for df in range(shards):
+        for dz in range(groups):
+            if df or dz:
+                peers.append((lax.rem(z + dz, groups), lax.rem(f + df, shards)))
+    me = z * shards + f
+    own = pltpu.make_async_copy(x_ref.at[me], o_ref.at[me], own_sem)
+    own.start()
+    greet([{"dp": pz, "fsdp": pf} for pz, pf in peers])
+    copies = []
+    for k, (pz, pf) in enumerate(peers):
+        copy = pltpu.make_async_remote_copy(
+            src_ref=x_ref.at[pz * shards + pf],
+            dst_ref=o_ref.at[me],
+            send_sem=send_sem.at[k],
+            recv_sem=recv_sem.at[k],
+            device_id={"dp": pz, "fsdp": pf},
+            device_id_type=MESH,
+        )
+        copy.start()
+        copies.append(copy)
+    own.wait()
+    for copy in copies:
+        copy.wait()
+
+
+def scatter(x, groups, shards):
+    count = groups * shards
+    return pl.pallas_call(
+        functools.partial(scatter_kernel, groups, shards),
+        out_shape=jax.ShapeDtypeStruct(x.shape, x.dtype),
+        in_specs=[ANY],
+        out_specs=ANY,
+        scratch_shapes=[
+            pltpu.SemaphoreType.DMA((count - 1,)),
+            pltpu.SemaphoreType.DMA((count - 1,)),
+            pltpu.SemaphoreType.DMA,
+        ],
+        compiler_params=pltpu.CompilerParams(collective_id=0, has_side_effects=True),
+    )(x)
+
+
+def exchange_kernel(shards, x_ref, o_ref, send_sem, recv_sem, own_sem):
+    f = lax.axis_index("fsdp")
+    own = pltpu.make_async_copy(x_ref.at[f], o_ref.at[f], own_sem)
+    own.start()
+    peers = [lax.rem(f + d, shards) for d in range(1, shards)]
+    greet([{"fsdp": p} for p in peers])
+    copies = []
+    for k, p in enumerate(peers):
+        copy = pltpu.make_async_remote_copy(
+            src_ref=x_ref.at[p],
+            dst_ref=o_ref.at[f],
+            send_sem=send_sem.at[k],
+            recv_sem=recv_sem.at[k],
+            device_id={"fsdp": p},
+            device_id_type=MESH,
+        )
+        copy.start()
+        copies.append(copy)
+    own.wait()
+    for copy in copies:
+        copy.wait()
+
+
+def exchange(x, shards, collective_id):
+    return pl.pallas_call(
+        functools.partial(exchange_kernel, shards),
+        out_shape=jax.ShapeDtypeStruct(x.shape, x.dtype),
+        in_specs=[ANY],
+        out_specs=ANY,
+        scratch_shapes=[
+            pltpu.SemaphoreType.DMA((shards - 1,)),
+            pltpu.SemaphoreType.DMA((shards - 1,)),
+            pltpu.SemaphoreType.DMA,
+        ],
+        compiler_params=pltpu.CompilerParams(
+            collective_id=collective_id, has_side_effects=True
+        ),
+    )(x)
+
+
+def gather_kernel(
+    groups, shards, sel_ref, root_ref, g_ref, r_ref, xs, xr, gs, gr, rs, rr, own_sem
+):
+    z, f = lax.axis_index("dp"), lax.axis_index("fsdp")
+    up, down = lax.rem(z + 1, groups), lax.rem(z + groups - 1, groups)
+    piece = sel_ref.shape[2]
+    half = root_ref.shape[1] // 2
+    own_root = pltpu.make_async_copy(root_ref, r_ref.at[z], own_sem.at[0])
+    own_root.start()
+    own_piece = pltpu.make_async_copy(
+        sel_ref.at[f], g_ref.at[z, :, pl.ds(f * piece, piece), :], own_sem.at[1]
+    )
+    own_piece.start()
+    peers = [lax.rem(f + d, shards) for d in range(1, shards)]
+    greet([{"fsdp": p} for p in peers] + [{"dp": up}, {"dp": down}])
+
+    def hop(buf, src, origin, part, way, send, recv, k):
+        rows = pl.ds(part * half, half)
+        return pltpu.make_async_remote_copy(
+            src_ref=(buf.at[origin] if src is None else src).at[:, rows, :],
+            dst_ref=buf.at[origin].at[:, rows, :],
+            send_sem=send.at[k],
+            recv_sem=recv.at[k],
+            device_id={"dp": way},
+            device_id_type=MESH,
+        )
+
+    def first(buf, src, send, recv):
+        moves = [
+            hop(buf, src, z, 0, up, send, recv, 0),
+            hop(buf, src, z, 1, down, send, recv, 1),
+            hop(buf, src, z, 1, up, send, recv, 2),
+            hop(buf, src, z, 0, down, send, recv, 3),
+        ]
+        for move in moves:
+            move.start()
+        return moves
+
+    def second(buf, send, recv):
+        return [
+            hop(buf, None, down, 0, up, send, recv, 4),
+            hop(buf, None, up, 1, down, send, recv, 5),
+        ]
+
+    root_first = first(r_ref, root_ref, rs, rr)
+    pieces = []
+    for k, p in enumerate(peers):
+        copy = pltpu.make_async_remote_copy(
+            src_ref=sel_ref.at[p],
+            dst_ref=g_ref.at[z, :, pl.ds(f * piece, piece), :],
+            send_sem=xs.at[k],
+            recv_sem=xr.at[k],
+            device_id={"fsdp": p},
+            device_id_type=MESH,
+        )
+        copy.start()
+        pieces.append(copy)
+    root_second = second(r_ref, rs, rr)
+    for near, far in zip(root_first[:2], root_second):
+        near.wait_recv()
+        far.start()
+    own_piece.wait()
+    for copy in pieces:
+        copy.wait()
+    block_first = first(g_ref, None, gs, gr)
+    block_second = second(g_ref, gs, gr)
+    for near, far in zip(block_first[:2], block_second):
+        near.wait_recv()
+        far.start()
+    for moves in (root_first, block_first):
+        for k, move in enumerate(moves):
+            if k >= 2:
+                move.wait_recv()
+            move.wait_send()
+    for move in root_second + block_second:
+        move.wait()
+    own_root.wait()
+
+
+def gather(sel, root, groups, shards):
+    whole = jax.ShapeDtypeStruct((groups,) + root.shape, root.dtype)
+    return pl.pallas_call(
+        functools.partial(gather_kernel, groups, shards),
+        out_shape=(whole, whole),
+        in_specs=[ANY, ANY],
+        out_specs=(ANY, ANY),
+        scratch_shapes=[pltpu.SemaphoreType.DMA((shards - 1,))] * 2
+        + [pltpu.SemaphoreType.DMA((6,))] * 4
+        + [pltpu.SemaphoreType.DMA((2,))],
+        compiler_params=pltpu.CompilerParams(collective_id=1, has_side_effects=True),
+    )(sel, root)
+
+
+def pick_blocks_kernel(groups, shards, slots, width, block_ref, occupied_ref, x_ref, o_ref):
+    def body(s, carry):
+        block = block_ref[s]
+        band = block // (x_ref.shape[2] // width)
+        column = pl.multiple_of(block % (x_ref.shape[2] // width) * width, width)
+        total = x_ref[band, :, pl.ds(column, width)].astype(F32)
+        for g in range(1, groups):
+            total += x_ref[g * shards + band, :, pl.ds(column, width)].astype(F32)
+        kept = jnp.where(occupied_ref[s] != 0, total, 0.0)
+        o_ref[s] = kept.astype(o_ref.dtype)
+        return carry
+
+    lax.fori_loop(0, slots, body, 0)
+
+
+def pick_blocks(block_of, occupied, x, groups, shards, slots, width):
+    piece, model = x.shape[1:]
+    step = 16 if piece % 16 == 0 else piece
+    return pl.pallas_call(
+        functools.partial(pick_blocks_kernel, groups, shards, slots, width),
+        grid=(piece // step,),
+        out_shape=jax.ShapeDtypeStruct((slots, piece, width), x.dtype),
+        in_specs=[SMEM, SMEM, pl.BlockSpec((groups * shards, step, model), lambda i: (0, i, 0))],
+        out_specs=pl.BlockSpec((slots, step, width), lambda i: (0, i, 0)),
+    )(block_of, occupied, x)
+
+
+def pick_home_kernel(per_band, slot_ref, x_ref, o_ref):
+    width = x_ref.shape[2]
+
+    def body(f, carry):
+        for c in range(per_band):
+            o_ref[f, :, c * width : (c + 1) * width] = x_ref[slot_ref[f * per_band + c]]
+        return carry
+
+    lax.fori_loop(0, o_ref.shape[0], body, 0)
+
+
+def pick_home(slot_table, x, bands, per_band):
+    slots, piece, width = x.shape
+    return pl.pallas_call(
+        functools.partial(pick_home_kernel, per_band),
+        out_shape=jax.ShapeDtypeStruct((bands, piece, per_band * width), x.dtype),
+        in_specs=[SMEM, VMEM],
+        out_specs=VMEM,
+    )(slot_table, x)
+
+
+def step_kernel(place_ref, g_ref, r_ref, l_ref, ls_ref, rs_ref, d_ref, ln_ref, rn_ref):
+    z = place_ref[0]
+    size = g_ref.shape[3]
+    rows = l_ref.shape[1]
+    block = g_ref[:, 0].reshape(size, size)
+    mine = g_ref[z, 0]
+    columns = g_ref[:, 0, :, pl.ds(pl.multiple_of(z * rows, rows), rows)].reshape(size, rows)
+    left = lax.dot_general(mine, block, (((1,), (1,)), ((), ())), preferred_element_type=F32)
+    ln_ref[0] = ls_ref[0] + left / size
+    right = lax.dot_general(columns, block, (((0,), (0,)), ((), ())), preferred_element_type=F32)
+    rn_ref[0] = rs_ref[0] + right / size
+    mixed = jnp.dot(l_ref[0], block, preferred_element_type=F32).astype(BF16)
+    root = r_ref[:, 0].reshape(size, size)
+    out = jnp.dot(mixed, root, preferred_element_type=F32).astype(d_ref.dtype)
+    d_ref[:, 0] = out.reshape(d_ref.shape[0], d_ref.shape[2], size)
+
+
+def step(place, g, r, left_root, left_state, right_state, shards):
+    groups, slots, rows, size = g.shape
+    piece = rows // shards
+    whole = pl.BlockSpec((groups, 1, rows, size), lambda m: (0, m, 0, 0))
+    strip = pl.BlockSpec((1, rows, size), lambda m: (m, 0, 0))
+    state = jax.ShapeDtypeStruct((slots, rows, size), F32)
+    return pl.pallas_call(
+        step_kernel,
+        grid=(slots,),
+        out_shape=(jax.ShapeDtypeStruct((shards, slots, piece, size), BF16), state, state),
+        in_specs=[SMEM, whole, whole, strip, strip, strip],
+        out_specs=(pl.BlockSpec((shards, 1, piece, size), lambda m: (0, m, 0, 0)), strip, strip),
+    )(place, g, r, left_root, left_state, right_state)
+
+
+def by_pieces(replica_grads, slot_table, left_gram_state, right_gram_state, left_inverse_root, right_inverse_root):
+    slots_here, _, _, rows, size = left_gram_state.shape
+    band_rows, model_width = replica_grads.shape[1:]
+    per_band = model_width // size
+    shards, groups = lax.axis_size("fsdp"), lax.axis_size("dp")
+    total_slots = shards * slots_here
+    piece = rows // shards
+    holder = slot_table[None, :] == jnp.arange(total_slots, dtype=jnp.int32)[:, None]
+    occupied = jnp.any(holder, axis=1).astype(jnp.int32)
+    numbers = jnp.arange(slot_table.shape[0], dtype=jnp.int32)
+    block_of = jnp.sum(jnp.where(holder, numbers[None, :], 0), axis=1).astype(jnp.int32)
+
+    arrived = scatter(
+        replica_grads.reshape(groups * shards, piece, model_width), groups, shards
+    )
+    chosen = pick_blocks(block_of, occupied, arrived, groups, shards, total_slots, size)
+    blocks, roots = gather(
+        chosen.reshape(shards, slots_here, piece, size),
+        right_inverse_root.reshape(slots_here, rows, size),
+        groups,
+        shards,
+    )
+    place = lax.axis_index("dp").astype(jnp.int32)[None]
+    outcome, left_new, right_new = step(
+        place,
+        blocks,
+        roots,
+        left_inverse_root.reshape(slots_here, rows, size),
+        left_gram_state.reshape(slots_here, rows, size),
+        right_gram_state.reshape(slots_here, rows, size),
+        shards,
+    )
+    returned = exchange(outcome, shards, 2)
+    homeward = pick_home(
+        slot_table, returned.reshape(total_slots, piece, size), shards, per_band
+    )
+    direction = exchange(homeward, shards, 3)
+    return (
+        direction.reshape(1, 1, rows, model_width),
+        left_new.reshape(left_gram_state.shape),
+        right_new.reshape(right_gram_state.shape),
+    )
+
+
+def fits_pieces(mesh_shape, grads, state):
+    groups, shards = mesh_shape["dp"], mesh_shape["fsdp"]
+    rows, size = state[3], state[4]
+    return (
+        groups == 4
+        and state[1] == 1
+        and grads[1] // shards == size
+        and rows % (shards * 16) == 0
+        and rows * groups == size
+    )
 
 
 def on_device(
@@ -106,14 +437,22 @@
         P("fsdp", None, "dp", None, None),
         P("fsdp", None, "dp", None, None),
     )
-    return jax.shard_map(
-        on_device,
-        mesh=mesh,
-        in_specs=placed,
-        out_specs=(
-            P("fsdp", "dp", None, None),
-            P("fsdp", None, "dp", None, None),
-            P("fsdp", None, "dp", None, None),
-        ),
-        check_vma=False,
-    )
+    places = (
+        P("fsdp", "dp", None, None),
+        P("fsdp", None, "dp", None, None),
+        P("fsdp", None, "dp", None, None),
+    )
+
+    def run(*args):
+        grads, _, state = args[:3]
+        fits = fits_pieces(mesh.shape, grads.shape, state.shape)
+        mapped = jax.shard_map(
+            by_pieces if fits else on_device,
+            mesh=mesh,
+            in_specs=placed,
+            out_specs=places,
+            check_vma=False,
+        )
+        return mapped(*args)
+
+    return run

time: 980 us -> 625 us (0.64)
  waiting for transfers between devices: 722 us -> 0 us
  Pallas kernels: 0 us -> 618 us
  local copies, waits for them, and re-layouts: 129 us -> 3.13 us
  matrix products: 60.5 us -> 0 us
  other arithmetic: 40.4 us -> 2.49 us
  between operations: 13.9 us -> 0.67 us
    pallas_call x0 -> x7, Pallas kernels: none -> 618 us  [the longest x1 347 us: gather(): pl.pallas_call(functools.partial(gather_kernel, groups, shards), out_shap...]
    all_gather x3 -> x0, waiting for transfers between devices: 416 us -> none  [the longest x1 183 us: on_device(): lax.all_gather(owned_rows, 'dp', axis=2, tiled=True)]
    all_to_all x1 -> x0, waiting for transfers between devices: 157 us -> none  [on_device(): lax.all_to_all(homeward, 'fsdp', split_axis=0, concat_axis=0, tiled=True)]
    reduce_scatter x1 -> x0, waiting for transfers between devices: 149 us -> none  [on_device(): lax.psum_scatter(replica_grads[0].astype(jnp.float32).astype(jnp.bfloat16...]
    dot_general x5 -> x0, matrix products: 60.5 us -> none  [the longest x1 21.6 us: on_device(): jnp.einsum('cn,ntb->tcb', chooser, returned.reshape(total_slots, strip_ro...]
    scatter x11 -> x0, other arithmetic: 36.5 us -> none
    all_gather x2 -> x0, local copies, waits for them, and re-layouts: 27 us -> none  [on_device(): lax.all_gather(owned_rows, 'dp', axis=2, tiled=True)]
    reshape x2 -> x0, local copies, waits for them, and re-layouts: 22 us -> none  [the longest x1 17.6 us: on_device(): lax.all_gather(owned_rows, 'dp', axis=2, tiled=True)]
  transfers between devices with their start and end apart: 5 -> 0, of which waited for: 5 -> 0; matrix products, arithmetic and copies ran while one was open for 12% -> 0% of each run, Pallas kernels for 0% -> 0%
where the time goes in v1:
time: 625 us; the launch traced here: 624 us
  Pallas kernels  618 us (99%)
    pallas_call x1, Pallas kernels, gather(): pl.pallas_call(functools.partial(gather_kernel, groups, shards), out_shap...  347 us
    pallas_call x1, Pallas kernels, scatter(): pl.pallas_call(functools.partial(scatter_kernel, groups, shards), out_sha...  183 us
    pallas_call x2, Pallas kernels, exchange(): pl.pallas_call(functools.partial(exchange_kernel, shards), out_shape=jax....  57.9 us
    pallas_call x1, Pallas kernels, step(): pl.pallas_call(step_kernel, grid=(slots,), out_shape=(jax.ShapeDtypeStruc...  21.3 us

profile of v1, /device:TPU:1, one launch (start us, length us, event | category | flops | bytes accessed | tf_op | source)
XLA Modules:
  0.0 624.5 jit_solution(6474991626462748637)
XLA Ops:
  0.6 0.7 fusion
  1.4 0.5 convert_element_type.3.occupied_ref
  1.9 1.3 select_reduce_fusion.block_ref
  3.1 183.1 %shard_map.85.x_ref = bf16[32,32,4096]{2,1,0:T(8,128)(2,1)} custom-call(bf16[32,32,4096]{2,1,0:T(8,128)(2,1)} %bitcast.17), custom_call_target="tpu_custom_call" | custom-call | tf_op jit(solution)/shard_map/pallas_call | solution.py:55
  186.3 6.1 shard_map.86
  192.3 346.6 %shard_map.87 = (bf16[4,5,256,1024]{3,2,1,0:T(8,128)(2,1)}, bf16[4,5,256,1024]{3,2,1,0:T(8,128)(2,1)}) custom-call(bf16[8,5,32,1024]{3,2,1,0:T(8,128)(2,1)} %bitcast.16, bf16[5,256,1024]{2,1,0:T(8,128)(2,1)} %bitcast.22), custom_call_target="tpu_custom_call" | custom-call | tf_op jit(solution)/shard_map/pallas_call | solution.py:190
  538.9 21.3 %shard_map.88 = (bf16[8,5,32,1024]{3,2,1,0:T(8,128)(2,1)}, f32[5,256,1024]{2,1,0:T(8,128)}, f32[5,256,1024]{2,1,0:T(8,128)}) custom-call(s32[1]{0:T(128)} %bitcast.place_ref, bf16[4,5,256,1024]{3,2,1,0:T(8,128)(2,1)} %get-tuple-element.8.g_ref, bf16[4,5,256,1024]{3,2,1,0:T(8,128)(2,1)} %get-tuple-element.9.r_ref, bf16[5,256,1024]{2,1,0:T(8,128)(2,1)} %bitcast.21, ...), custom_call_target="tpu_custom_call" | custom-call | tf_op jit(solution)/shard_map/pallas_call | solution.py:273
  560.2 31.6 %shard_map.89 = bf16[8,5,32,1024]{3,2,1,0:T(8,128)(2,1)} custom-call(bf16[8,5,32,1024]{3,2,1,0:T(8,128)(2,1)} %get-tuple-element.10.x_ref), custom_call_target="tpu_custom_call" | custom-call | tf_op jit(solution)/shard_map/pallas_call | solution.py:93
  591.9 3.3 shard_map.90.x_ref
  595.1 26.2 %shard_map.91 = bf16[8,32,4096]{2,1,0:T(8,128)(2,1)} custom-call(bf16[8,32,4096]{2,1,0:T(8,128)(2,1)} %shard_map.90.x_ref), custom_call_target="tpu_custom_call" | custom-call | tf_op jit(solution)/shard_map/pallas_call | solution.py:93
  621.4 3.1 copy.14

commit v2 on v1

--- a/solution.py
+++ b/solution.py
@@ -22,7 +22,58 @@
     pl.semaphore_wait(barrier, len(peers))
 
 
-def scatter_kernel(groups, shards, x_ref, o_ref, send_sem, recv_sem, own_sem):
+def chain_start(groups, z, buf, src, send, recv):
+    def move(origin, way, side, d):
+        origin = jnp.clip(origin, 0, groups - 1)
+        return pltpu.make_async_remote_copy(
+            src_ref=src if d == 0 and src is not None else buf.at[origin],
+            dst_ref=buf.at[origin],
+            send_sem=send.at[side, d],
+            recv_sem=recv.at[side, d],
+            device_id={"dp": jnp.clip(way, 0, groups - 1)},
+            device_id_type=MESH,
+        )
+
+    sides = ((0, -1), (1, 1))
+
+    def send_on(d):
+        for side, sign in sides:
+            origin, way = z + sign * d, z - sign
+            inside = (origin >= 0) & (origin < groups) & (way >= 0) & (way < groups)
+
+            @pl.when(inside)
+            def _():
+                move(origin, way, side, d).start()
+
+    def relay():
+        for d in range(1, groups):
+            for side, sign in sides:
+                origin = z + sign * d
+
+                @pl.when((origin >= 0) & (origin < groups))
+                def _():
+                    move(origin, z, side, d - 1).wait_recv()
+
+            if d < groups - 1:
+                send_on(d)
+
+    def finish():
+        for d in range(groups - 1):
+            for side, sign in sides:
+                origin, way = z + sign * d, z - sign
+                inside = (origin >= 0) & (origin < groups) & (way >= 0) & (way < groups)
+
+                @pl.when(inside)
+                def _():
+                    move(origin, way, side, d).wait_send()
+
+    send_on(0)
+    return relay, finish
+
+
+def scatter_kernel(
+    groups, shards, x_ref, root_ref, o_ref, near_ref, send_sem, recv_sem, rs, rr, own_sem
+):
     z, f = lax.axis_index("dp"), lax.axis_index("fsdp")
     peers = []
     for df in range(shards):
@@ -45,25 +96,32 @@
         )
         copy.start()
         copies.append(copy)
+    root = pltpu.make_async_remote_copy(
+        src_ref=root_ref,
+        dst_ref=near_ref,
+        send_sem=rs,
+        recv_sem=rr,
+        device_id={"dp": z + 1 - 2 * lax.rem(z, 2)},
+        device_id_type=MESH,
+    )
+    root.start()
     own.wait()
     for copy in copies:
         copy.wait()
-
-
-def scatter(x, groups, shards):
+    root.wait()
+
+
+def scatter(x, root, groups, shards):
     count = groups * shards
     return pl.pallas_call(
         functools.partial(scatter_kernel, groups, shards),
-        out_shape=jax.ShapeDtypeStruct(x.shape, x.dtype),
-        in_specs=[ANY],
-        out_specs=ANY,
-        scratch_shapes=[
-            pltpu.SemaphoreType.DMA((count - 1,)),
-            pltpu.SemaphoreType.DMA((count - 1,)),
-            pltpu.SemaphoreType.DMA,
-        ],
+        out_shape=(jax.ShapeDtypeStruct(x.shape, x.dtype), jax.ShapeDtypeStruct(root.shape, root.dtype)),
+        in_specs=[ANY, ANY],
+        out_specs=(ANY, ANY),
+        scratch_shapes=[pltpu.SemaphoreType.DMA((count - 1,))] * 2
+        + [pltpu.SemaphoreType.DMA] * 3,
         compiler_params=pltpu.CompilerParams(collective_id=0, has_side_effects=True),
-    )(x)
+    )(x, root)
 
 
 def exchange_kernel(shards, x_ref, o_ref, send_sem, recv_sem, own_sem):
@@ -107,51 +165,49 @@
 
 
 def gather_kernel(
-    groups, shards, sel_ref, root_ref, g_ref, r_ref, xs, xr, gs, gr, rs, rr, own_sem
+    groups, shards, sel_ref, root_ref, near_ref, g_ref, r_ref, xs, xr, gs, gr, rs, rr, own_sem
 ):
     z, f = lax.axis_index("dp"), lax.axis_index("fsdp")
-    up, down = lax.rem(z + 1, groups), lax.rem(z + groups - 1, groups)
     piece = sel_ref.shape[2]
-    half = root_ref.shape[1] // 2
-    own_root = pltpu.make_async_copy(root_ref, r_ref.at[z], own_sem.at[0])
+    pair = z + 1 - 2 * lax.rem(z, 2)
+    middle = (z > 0) & (z < groups - 1)
+    across = groups - 1 - z
+    far = jnp.where(middle, across, groups - 1 - pair)
+    far_pair = far + 1 - 2 * lax.rem(far, 2)
+    own = pltpu.make_async_copy(
+        sel_ref.at[f], g_ref.at[z, :, pl.ds(f * piece, piece), :], own_sem.at[0]
+    )
+    own.start()
+    own_root = pltpu.make_async_copy(root_ref, r_ref.at[z], own_sem.at[1])
     own_root.start()
-    own_piece = pltpu.make_async_copy(
-        sel_ref.at[f], g_ref.at[z, :, pl.ds(f * piece, piece), :], own_sem.at[1]
-    )
-    own_piece.start()
-    peers = [lax.rem(f + d, shards) for d in range(1, shards)]
-    greet([{"fsdp": p} for p in peers] + [{"dp": up}, {"dp": down}])
-
-    def hop(buf, src, origin, part, way, send, recv, k):
-        rows = pl.ds(part * half, half)
+    near_root = pltpu.make_async_copy(near_ref, r_ref.at[pair], own_sem.at[2])
+    near_root.start()
+
+    def hand(src, row, way, k, sent):
         return pltpu.make_async_remote_copy(
-            src_ref=(buf.at[origin] if src is None else src).at[:, rows, :],
-            dst_ref=buf.at[origin].at[:, rows, :],
-            send_sem=send.at[k],
-            recv_sem=recv.at[k],
+            src_ref=src,
+            dst_ref=r_ref.at[row],
+            send_sem=rs.at[sent],
+            recv_sem=rr.at[k],
             device_id={"dp": way},
             device_id_type=MESH,
         )
 
-    def first(buf, src, send, recv):
-        moves = [
-            hop(buf, src, z, 0, up, send, recv, 0),
-            hop(buf, src, z, 1, down, send, recv, 1),
-            hop(buf, src, z, 1, up, send, recv, 2),
-            hop(buf, src, z, 0, down, send, recv, 3),
-        ]
-        for move in moves:
-            move.start()
-        return moves
-
-    def second(buf, send, recv):
-        return [
-            hop(buf, None, down, 0, up, send, recv, 4),
-            hop(buf, None, up, 1, down, send, recv, 5),
-        ]
-
-    root_first = first(r_ref, root_ref, rs, rr)
-    pieces = []
+    swaps = [hand(root_ref, z, across, 0, 0), hand(near_ref, pair, across, 1, 1)]
+    passes = [
+        hand(r_ref.at[far], far, pair, 0, 2),
+        hand(r_ref.at[far_pair], far_pair, pair, 1, 3),
+    ]
+    peers = [lax.rem(f + d, shards) for d in range(1, shards)]
+    near = [lax.rem(z + 1, groups), lax.rem(z + groups - 1, groups)]
+    greet([{"fsdp": p} for p in peers] + [{"dp": p} for p in near])
+
+    @pl.when(middle)
+    def _():
+        for swap in swaps:
+            swap.start()
+
+    copies = []
     for k, p in enumerate(peers):
         copy = pltpu.make_async_remote_copy(
             src_ref=sel_ref.at[p],
@@ -162,41 +218,44 @@
             device_id_type=MESH,
         )
         copy.start()
-        pieces.append(copy)
-    root_second = second(r_ref, rs, rr)
-    for near, far in zip(root_first[:2], root_second):
-        near.wait_recv()
-        far.start()
-    own_piece.wait()
-    for copy in pieces:
+        copies.append(copy)
+    for onward in passes:
+        onward.wait_recv()
+
+        @pl.when(middle)
+        def _():
+            onward.start()
+
+    own.wait()
+    for copy in copies:
         copy.wait()
-    block_first = first(g_ref, None, gs, gr)
-    block_second = second(g_ref, gs, gr)
-    for near, far in zip(block_first[:2], block_second):
-        near.wait_recv()
-        far.start()
-    for moves in (root_first, block_first):
-        for k, move in enumerate(moves):
-            if k >= 2:
-                move.wait_recv()
+    relay, finish = chain_start(groups, z, g_ref, None, gs, gr)
+    relay()
+    finish()
+
+    @pl.when(middle)
+    def _():
+        for move in swaps + passes:
             move.wait_send()
-    for move in root_second + block_second:
-        move.wait()
+
     own_root.wait()
-
-
-def gather(sel, root, groups, shards):
-    whole = jax.ShapeDtypeStruct((groups,) + root.shape, root.dtype)
+    near_root.wait()
+
+
+def gather(sel, root, near, groups, shards):
+    slots, piece, size = sel.shape[1:]
+    whole = jax.ShapeDtypeStruct((groups, slots, shards * piece, size), sel.dtype)
     return pl.pallas_call(
         functools.partial(gather_kernel, groups, shards),
         out_shape=(whole, whole),
-        in_specs=[ANY, ANY],
+        in_specs=[ANY] * 3,
         out_specs=(ANY, ANY),
         scratch_shapes=[pltpu.SemaphoreType.DMA((shards - 1,))] * 2
-        + [pltpu.SemaphoreType.DMA((6,))] * 4
-        + [pltpu.SemaphoreType.DMA((2,))],
+        + [pltpu.SemaphoreType.DMA((2, groups - 1))] * 2
+        + [pltpu.SemaphoreType.DMA((4,)), pltpu.SemaphoreType.DMA((2,))]
+        + [pltpu.SemaphoreType.DMA((3,))],
         compiler_params=pltpu.CompilerParams(collective_id=1, has_side_effects=True),
-    )(sel, root)
+    )(sel, root, near)
 
 
 def pick_blocks_kernel(groups, shards, slots, width, block_ref, occupied_ref, x_ref, o_ref):
@@ -291,15 +350,16 @@
     numbers = jnp.arange(slot_table.shape[0], dtype=jnp.int32)
     block_of = jnp.sum(jnp.where(holder, numbers[None, :], 0), axis=1).astype(jnp.int32)
 
-    arrived = scatter(
-        replica_grads.reshape(groups * shards, piece, model_width), groups, shards
+    own_roots = right_inverse_root.reshape(slots_here, rows, size)
+    arrived, near_roots = scatter(
+        replica_grads.reshape(groups * shards, piece, model_width),
+        own_roots,
+        groups,
+        shards,
     )
     chosen = pick_blocks(block_of, occupied, arrived, groups, shards, total_slots, size)
     blocks, roots = gather(
-        chosen.reshape(shards, slots_here, piece, size),
-        right_inverse_root.reshape(slots_here, rows, size),
-        groups,
-        shards,
+        chosen.reshape(shards, slots_here, piece, size), own_roots, near_roots, groups, shards
     )
     place = lax.axis_index("dp").astype(jnp.int32)[None]
     outcome, left_new, right_new = step(

time: 625 us -> 640 us (1.024)
  Pallas kernels: 618 us -> 633 us
    pallas_call x1, Pallas kernels: 183 us -> 200 us  [scatter(): pl.pallas_call(functools.partial(scatter_kernel, groups, shards), out_sha...]
where the time goes in v2:
time: 640 us; the launch traced here: 639 us
  Pallas kernels  633 us (99%)
    pallas_call x1, Pallas kernels, gather(): pl.pallas_call(functools.partial(gather_kernel, groups, shards), out_shap...  341 us
    pallas_call x1, Pallas kernels, scatter(): pl.pallas_call(functools.partial(scatter_kernel, groups, shards), out_sha...  200 us
    pallas_call x2, Pallas kernels, exchange(): pl.pallas_call(functools.partial(exchange_kernel, shards), out_shape=jax....  62 us
    pallas_call x1, Pallas kernels, step(): pl.pallas_call(step_kernel, grid=(slots,), out_shape=(jax.ShapeDtypeStruc...  21.3 us

profile of v2, /device:TPU:1, one launch (start us, length us, event | category | flops | bytes accessed | tf_op | source)
XLA Modules:
  0.0 639.4 jit_solution(5316107896892163110)
XLA Ops:
  0.6 0.7 fusion
  1.4 0.5 convert_element_type.3.occupied_ref
  1.9 1.3 select_reduce_fusion.block_ref
  3.1 200.0 %shard_map.85 = (bf16[32,32,4096]{2,1,0:T(8,128)(2,1)}, bf16[5,256,1024]{2,1,0:T(8,128)(2,1)}) custom-call(bf16[32,32,4096]{2,1,0:T(8,128)(2,1)} %bitcast.19, bf16[5,256,1024]{2,1,0:T(8,128)(2,1)} %bitcast.16), custom_call_target="tpu_custom_call" | custom-call | tf_op jit(solution)/shard_map/pallas_call | solution.py:116
  203.1 6.1 shard_map.86
  209.1 340.6 %shard_map.87 = (bf16[4,5,256,1024]{3,2,1,0:T(8,128)(2,1)}, bf16[4,5,256,1024]{3,2,1,0:T(8,128)(2,1)}) custom-call(bf16[8,5,32,1024]{3,2,1,0:T(8,128)(2,1)} %bitcast.18, bf16[5,256,1024]{2,1,0:T(8,128)(2,1)} %bitcast.17, bf16[5,256,1024]{2,1,0:T(8,128)(2,1)} %get-tuple-element.11.near_ref), custom_call_target="tpu_custom_call" | custom-call | tf_op jit(solution)/shard_map/pallas_call | solution.py:248
  549.7 21.3 %shard_map.88 = (bf16[8,5,32,1024]{3,2,1,0:T(8,128)(2,1)}, f32[5,256,1024]{2,1,0:T(8,128)}, f32[5,256,1024]{2,1,0:T(8,128)}) custom-call(s32[1]{0:T(128)} %bitcast.place_ref, bf16[4,5,256,1024]{3,2,1,0:T(8,128)(2,1)} %get-tuple-element.12.g_ref, bf16[4,5,256,1024]{3,2,1,0:T(8,128)(2,1)} %get-tuple-element.13.r_ref, bf16[5,256,1024]{2,1,0:T(8,128)(2,1)} %bitcast.23, ...), custom_call_target="tpu_custom_call" | custom-call | tf_op jit(solution)/shard_map/pallas_call | solution.py:332
  571.1 35.8 %shard_map.89 = bf16[8,5,32,1024]{3,2,1,0:T(8,128)(2,1)} custom-call(bf16[8,5,32,1024]{3,2,1,0:T(8,128)(2,1)} %get-tuple-element.14.x_ref), custom_call_target="tpu_custom_call" | custom-call | tf_op jit(solution)/shard_map/pallas_call | solution.py:151
  606.8 3.3 shard_map.90.x_ref
  610.1 26.2 %shard_map.91 = bf16[8,32,4096]{2,1,0:T(8,128)(2,1)} custom-call(bf16[8,32,4096]{2,1,0:T(8,128)(2,1)} %shard_map.90.x_ref), custom_call_target="tpu_custom_call" | custom-call | tf_op jit(solution)/shard_map/pallas_call | solution.py:151
  636.3 3.1 copy.14
